TPU v7x, 32 devices: a 4x2x2 block of a 4x4x8 slice. The times are simulated.
32 devices in a mesh: dp: 4 (over y, z), tp: 8 (over x, core).
Axes of the slice: x: 4, y: 2, z: 2, core: 2. Of those that a mesh axis runs over, the one named last changes fastest.
The devices are a block of a 4x4x8 slice.
Arguments:
- hidden: bfloat16 [4, 16, 2048], P('dp'), parts along dimension 0
- norm_w: bfloat16 [2048], replicated
- embedding: bfloat16 [256000, 2048], P('tp')
- draft_ids: int32 [4, 16], P('dp'), parts along dimension 0
Outputs:
- output 1: float32 [4, 16], P('dp'), parts along dimension 0
- output 2: float32 [4, 16], P('dp'), parts along dimension 0
There are 4 independent parts. A program takes and returns all parts, laid end to end along the dimension named above; an argument that names none is the same for every part.
All inputs are finite; a program needn't handle non-finite values.
Results may differ from a plain program's by a relative error of at most 0.001.
Values sent between devices are 32-bit elements.
A program may use at most 768 MiB of HBM per device.

v0:
```python
import jax
import jax.numpy as jnp
from jax import lax
from jax.sharding import PartitionSpec as P, NamedSharding

EPS = 1e-6


def solution(mesh):
    def local_part(hidden, norm_w, embedding, draft_ids):
        shard_rows = embedding.shape[0]
        offset = lax.axis_index("tp") * shard_rows
        x_float = hidden.astype(jnp.float32)
        mean_sq = jnp.mean(x_float * x_float, axis=-1, keepdims=True)
        normed = (x_float * lax.rsqrt(mean_sq + EPS) * (1.0 + norm_w.astype(jnp.float32))).astype(jnp.bfloat16)
        logits = jnp.einsum("bgd,vd->bgv", normed, embedding, preferred_element_type=jnp.float32)
        local_max = jnp.max(logits, axis=-1)
        row_max = lax.pmax(local_max, "tp")
        exp_shift = jnp.exp(logits - row_max[..., None])
        exp_total = lax.psum(jnp.sum(exp_shift, axis=-1), "tp")
        weighted = lax.psum(jnp.sum(exp_shift * logits, axis=-1), "tp")
        local_ids = draft_ids - offset
        is_owned = (local_ids >= 0) & (local_ids < shard_rows)
        safe_ids = jnp.clip(local_ids, 0, shard_rows - 1)
        local_pick = jnp.take_along_axis(logits, safe_ids[..., None], axis=-1)[..., 0]
        picked = lax.psum(jnp.where(is_owned, local_pick, 0.0), "tp")
        log_norm = row_max + jnp.log(exp_total)
        return picked - log_norm, log_norm - weighted / exp_total

    return jax.shard_map(local_part, mesh=mesh, in_specs=(P("dp", None, None), P(None), P("tp", None), P("dp", None)), out_specs=(P("dp", None), P("dp", None)), check_vma=False)
```

profile of v0, /device:TPU:81, one launch (start us, length us, event | category | flops | bytes accessed | tf_op | source)
XLA Modules:
  0.0 78.6 jit_solution(14682803268582000314)
XLA Ops:
  0.6 0.7 convert_add_fusion
  1.3 1.0 %fusion.1 = f32[16]{0:T(128)S(1)} fusion(bf16[1,16,2048]{2,1,0:T(8,128)(2,1)} %param.4), kind=kLoop, calls=%fused_computation.6 | loop fusion | flops 98288 | bytes 65600 | tf_op jit(solution)/shard_map/reduce_sum | solution.py:14
  2.3 45.8 %fusion.10 = (f32[16]{0:T(128)S(1)}, f32[16,32000]{1,0:T(8,128)S(1)}) fusion(bf16[32000,2048]{1,0:T(8,128)(2,1)} %param.6, bf16[1,16,2048]{2,1,0:T(8,128)(2,1)} %param.4, f32[2048]{0:T(1024)S(1)} %convert_add_fusion, f32[16]{0:T(128)S(1)} %add_rsqrt_fusion), kind=kOutput, calls=%fused_computation.24 | convolution fusion | flops 2097795072 | bytes 133193856 | tf_op jit(solution)/shard_map/bgd,vd->bgv/dot_general | solution.py:16
  48.1 0.0 copy-start
  48.1 13.9 %pmax.7 = f32[1,16]{1,0:T(1,128)S(1)} all-reduce(f32[1,16]{1,0:T(1,128)S(1)} %bitcast.24), channel_id=1, replica_groups=mesh['dp'=4,'tp'=8] {'tp'}, use_global_device_ids=true, to_apply=%region_3.0 | all-reduce | flops 16 | bytes 128 | tf_op jit(solution)/shard_map/pmax | solution.py:18
  61.9 0.9 %multiply_reduce_fusion = (f32[16]{0:T(128)S(1)}, f32[16]{0:T(128)S(1)}) fusion(f32[16,32000]{1,0:T(8,128)S(1)} %get-tuple-element.10, f32[16]{0:T(128)S(1)} %bitcast.21), kind=kLoop, calls=%fused_computation.1 | loop fusion | flops 2047968 | bytes 2048192 | tf_op jit(solution)/shard_map/reduce_sum | solution.py:21
  62.8 0.0 copy-done
  62.9 0.7 gather_fusion
  63.6 14.5 %all-reduce = (f32[1,16]{1,0:T(1,128)S(1)}, f32[1,16]{1,0:T(1,128)S(1)}, f32[1,16]{1,0:T(1,128)S(1)}) all-reduce(f32[1,16]{1,0:T(1,128)S(1)} %and_select_fusion.1, f32[1,16]{1,0:T(1,128)S(1)} %bitcast.23, f32[1,16]{1,0:T(1,128)S(1)} %bitcast.22), channel_id=1, replica_groups=mesh['dp'=4,'tp'=8] {'tp'}, use_global_device_ids=true, to_apply=%region_1.0 | all-reduce | flops 48 | bytes 384 | tf_op jit(solution)/shard_map/psum | solution.py:26
  78.1 0.5 divide_subtract_fusion
  (6 shorter events, 0.1 us)
Async XLA Ops:
  48.1 14.8 %copy-start = (s32[1,16]{1,0:T(1,128)S(1)}, s32[1,16]{1,0:T(1,128)}, u32[]{:S(2)}) copy-start(s32[1,16]{1,0:T(1,128)} %param.7) | copy-start | bytes 196
where the time goes:
time: 79 us; the launch traced here: 78.6 us
  matrix products  45.8 us (58%)
  blocking collectives  28.4 us (36%)
  other arithmetic  3.12 us (4%)
    dot_general x1, matrix products, local_part(): jnp.einsum('bgd,vd->bgv', normed, embedding, preferred_element_type=jnp.f...  45.8 us
    psum x1, blocking collectives, local_part(): picked = lax.psum(jnp.where(is_owned, local_pick, 0.0), 'tp')  14.5 us
    pmax x1, blocking collectives, local_part(): row_max = lax.pmax(local_max, 'tp')  13.9 us

commit v1 on v0

v1 whole, which is shorter than its diff:
```python
import functools

import jax
import jax.numpy as jnp
from jax import lax
from jax.experimental import pallas as pl
from jax.experimental.pallas import tpu as pltpu
from jax.sharding import PartitionSpec as P

EPS = 1e-6
MESH = pl.DeviceIdType.MESH
LANES = 128
HALVES = 2
SHARE = 4
CHUNK_ROWS = 800


def head_kernel(
    group, tp, rows, hid_hbm, w_hbm, emb_hbm, ids_hbm, lp_ref, ent_ref,
    hid_v, w_v, ids_v, hx, ids_x, hb, ebuf, zs, sbuf, rbuf,
    in_sem, esem, h_send, h_recv, f_send, f_recv, id_send, id_recv, s_send, s_recv,
):
    npos, depth = hid_v.shape
    half = depth // HALVES
    chunk = CHUNK_ROWS
    nchunk = rows // chunk
    nsrc = group * tp

    dp_me = lax.axis_index("dp")
    tp_me = lax.axis_index("tp")
    q = lax.rem(dp_me, group)
    base = dp_me - q
    c = lax.rem(tp_me, 2)
    sibling = tp_me + 1 - 2 * c
    me = q * tp + tp_me

    def peer(r):
        return base + lax.rem(q + r, group)

    small = [
        pltpu.make_async_copy(hid_hbm.at[0], hid_v, in_sem.at[0]),
        pltpu.make_async_copy(w_hbm, w_v, in_sem.at[1]),
        pltpu.make_async_copy(ids_hbm, ids_v, in_sem.at[2]),
    ]
    for copy in small:
        copy.start()
    loads = []
    for j in range(nchunk):
        pair = []
        for o in range(HALVES):
            col = half * (c if o == 0 else 1 - c)
            copy = pltpu.make_async_copy(
                emb_hbm.at[pl.ds(q * rows + j * chunk, chunk), pl.ds(pl.multiple_of(col, half), half)],
                ebuf.at[o, pl.ds(j * chunk, chunk)],
                esem.at[j, o],
            )
            copy.start()
            pair.append(copy)
        loads.append(pair)

    barrier = pltpu.get_barrier_semaphore()
    for r in range(group):
        for t in range(tp):
            if r or t:
                pl.semaphore_signal(
                    barrier, inc=1, device_id=(peer(r), lax.rem(tp_me + t, tp)), device_id_type=MESH
                )

    for copy in small:
        copy.wait()
    x = hid_v[...].astype(jnp.float32)
    scale = lax.rsqrt(jnp.mean(x * x, axis=-1, keepdims=True) + EPS)
    h = (x * scale * (1.0 + w_v[...].astype(jnp.float32))).astype(jnp.bfloat16)
    h32 = h.astype(jnp.float32)
    for s in range(HALVES):
        hx[q, s] = h32[:, s * half:(s + 1) * half]
    ids_x[q] = jnp.concatenate([ids_v[...], jnp.full((1, LANES - npos), -1, jnp.int32)], axis=1)

    pl.semaphore_wait(barrier, nsrc - 1)

    direct, ident = [], []
    for r in range(1, group):
        copy = pltpu.make_async_remote_copy(
            src_ref=hx.at[q, c], dst_ref=hx.at[q, c], send_sem=h_send.at[r], recv_sem=h_recv.at[r],
            device_id=(peer(r), tp_me), device_id_type=MESH)
        copy.start()
        direct.append(copy)
    for r in range(1, group):
        copy = pltpu.make_async_remote_copy(
            src_ref=ids_x.at[q], dst_ref=ids_x.at[q], send_sem=id_send.at[r], recv_sem=id_recv.at[r],
            device_id=(peer(r), tp_me), device_id_type=MESH)
        copy.start()
        ident.append(copy)

    def place(p, o):
        col = c if o == 0 else 1 - c
        hb[o, pl.ds(pl.multiple_of(p * npos, npos), npos), :] = hx[p, col].astype(jnp.bfloat16)

    for o in range(HALVES):
        place(q, o)
    forward = []
    for r in range(1, group):
        p = lax.rem(q - r + group, group)
        direct[r - 1].wait_recv()
        copy = pltpu.make_async_remote_copy(
            src_ref=hx.at[p, c], dst_ref=hx.at[p, c], send_sem=f_send.at[r], recv_sem=f_recv.at[r],
            device_id=(dp_me, sibling), device_id_type=MESH)
        copy.start()
        forward.append(copy)
        place(p, 0)
    for copy in ident:
        copy.wait_recv()

    lane = lax.broadcasted_iota(jnp.int32, (8, LANES), 1)
    want = jnp.full((8, LANES), -1, jnp.int32)
    for p in range(group):
        moved = jnp.broadcast_to(ids_x[p], (8, LANES))
        if p:
            moved = pltpu.roll(moved, p * npos, 1)
        want = jnp.where((lane >= p * npos) & (lane < (p + 1) * npos), moved, want)
    first_row = tp_me * (rows * group) + q * rows
    want = want - first_row - lax.broadcasted_iota(jnp.int32, (8, LANES), 0)

    def score(j, o):
        return lax.dot_general(
            ebuf[o, j * chunk:(j + 1) * chunk, :], hb[o], (((1,), (1,)), ((), ())), preferred_element_type=jnp.float32)

    def stats(j, state):
        z = zs[j % 2].reshape(chunk // 8, 8, LANES)
        top = jnp.max(z, axis=0)
        row = lax.broadcasted_iota(jnp.int32, (chunk // 8, 8, LANES), 0) * 8 + j * chunk
        pick = jnp.sum(jnp.where(row == want[None], z, 0.0), axis=0)
        if state is not None:
            top = jnp.maximum(top, state[0])
        e = jnp.exp(z - top[None])
        total = jnp.sum(e, axis=0)
        weighted = jnp.sum(e * z, axis=0)
        if state is not None:
            fade = jnp.exp(state[0] - top)
            total = total + state[1] * fade
            weighted = weighted + state[2] * fade
            pick = pick + state[3]
        return top, total, weighted, pick

    for s in range(2):
        zs[s] = jnp.zeros((chunk, LANES), jnp.float32)
    state = None
    for j in range(nchunk):
        loads[j][0].wait()
        if j == 0:
            first = score(0, 0)
            for r in range(1, group):
                forward[r - 1].wait_recv()
                place(lax.rem(q - r + group, group), 1)
            loads[0][1].wait()
            zs[0, :, :group * npos] = first + score(0, 1)
        else:
            loads[j][1].wait()
            zs[j % 2, :, :group * npos] = score(j, 0) + score(j, 1)
            state = stats(j - 1, state)
    state = stats(nchunk - 1, state)

    top8, total8, weighted8, pick8 = state
    top = jnp.max(top8, axis=0, keepdims=True)
    fade = jnp.exp(top8 - top)
    full = lambda v: jnp.broadcast_to(v, (8, LANES))
    top = full(top)
    total = full(jnp.sum(total8 * fade, axis=0, keepdims=True))
    weighted = full(jnp.sum(weighted8 * fade, axis=0, keepdims=True))
    pick = full(jnp.sum(pick8, axis=0, keepdims=True))
    for p in range(group):
        message = jnp.zeros((8, LANES), jnp.float32)
        for at, v in ((0, top), (1, top), (4, total), (5, weighted), (6, pick)):
            shift = (at * npos - p * npos) % LANES
            moved = pltpu.roll(v, shift, 1) if shift else v
            message = jnp.where((lane >= at * npos) & (lane < (at + 1) * npos), moved, message)
        sbuf[p] = message[:1]

    for r in range(group):
        for t in range(tp):
            if r or t:
                pltpu.make_async_remote_copy(
                    src_ref=sbuf.at[lax.rem(q + r, group)], dst_ref=rbuf.at[me], send_sem=s_send, recv_sem=s_recv,
                    device_id=(peer(r), lax.rem(tp_me + t, tp)), device_id_type=MESH).start()
    rbuf[me] = sbuf[q]
    for copies in (direct, ident, forward):
        for copy in copies:
            copy.wait_send()
    everyone = pltpu.make_async_remote_copy(
        src_ref=rbuf.at[pl.ds(0, nsrc - 1)], dst_ref=rbuf.at[pl.ds(0, nsrc - 1)], send_sem=s_send, recv_sem=s_recv,
        device_id=(dp_me, tp_me), device_id_type=MESH)
    everyone.wait_recv()
    everyone.wait_send()

    got = rbuf[...]
    values = pltpu.roll(got, LANES // 2, 2)
    top = jnp.max(got, axis=0)
    sums = jnp.sum(jnp.exp(got - top[None]) * values, axis=0)
    total = sums[:, :npos]
    weighted = pltpu.roll(sums, LANES - npos, 1)[:, :npos]
    pick = pltpu.roll(sums, LANES - 2 * npos, 1)[:, :npos]
    log_norm = top[:, :npos] + jnp.log(total)
    lp_ref[...] = pick - log_norm
    ent_ref[...] = log_norm - weighted / total


def solution(mesh):
    tp = mesh.shape["tp"]
    group = next(n for n in (SHARE, 2, 1) if mesh.shape["dp"] % n == 0)

    def local_part(hidden, norm_w, embedding, draft_ids):
        npos, depth = hidden.shape[1:]
        rows = embedding.shape[0] // group
        half = depth // HALVES
        nchunk = rows // CHUNK_ROWS
        any_spec = pl.BlockSpec(memory_space=pl.ANY)
        dma = pltpu.SemaphoreType.DMA
        return pl.pallas_call(
            functools.partial(head_kernel, group, tp, rows),
            out_shape=[jax.ShapeDtypeStruct((1, npos), jnp.float32)] * 2,
            in_specs=[any_spec] * 4,
            out_specs=[pl.BlockSpec(memory_space=pltpu.VMEM)] * 2,
            scratch_shapes=[
                pltpu.VMEM((npos, depth), jnp.bfloat16),
                pltpu.VMEM((1, depth), jnp.bfloat16),
                pltpu.VMEM((1, npos), jnp.int32),
                pltpu.VMEM((group, HALVES, npos, half), jnp.float32),
                pltpu.VMEM((group, 1, LANES), jnp.int32),
                pltpu.VMEM((HALVES, group * npos, half), jnp.bfloat16),
                pltpu.VMEM((HALVES, rows, half), jnp.bfloat16),
                pltpu.VMEM((2, CHUNK_ROWS, LANES), jnp.float32),
                pltpu.VMEM((group, 1, LANES), jnp.float32),
                pltpu.VMEM((group * tp, 1, LANES), jnp.float32),
                dma((3,)), dma((nchunk, HALVES)),
                dma((group,)), dma((group,)), dma((group,)), dma((group,)), dma((group,)), dma((group,)),
                dma, dma,
            ],
            compiler_params=pltpu.CompilerParams(
                collective_id=0, has_side_effects=True, vmem_limit_bytes=60 * 2**20),
        )(hidden, norm_w.reshape(1, depth), embedding, draft_ids)

    return jax.shard_map(
        local_part, mesh=mesh,
        in_specs=(P("dp", None, None), P(None), P("tp", None), P("dp", None)),
        out_specs=(P("dp", None), P("dp", None)), check_vma=False)
```

time: 79 us -> 48.2 us (0.61)
  matrix products: 45.8 us -> 0 us
  Pallas kernels: 0 us -> 43.8 us
  blocking collectives: 28.4 us -> 0 us
  other arithmetic: 3.12 us -> 0 us
  local copies, waits for them, and re-layouts: 0.69 us -> 3.59 us
    dot_general x1 -> x0, matrix products: 45.8 us -> none  [local_part(): jnp.einsum('bgd,vd->bgv', normed, embedding, preferred_element_type=jnp.f...]
    pallas_call x0 -> x1, Pallas kernels: none -> 43.8 us  [local_part(): pl.pallas_call(functools.partial(head_kernel, group, tp, rows), out_shape...]
    psum x1 -> x0, blocking collectives: 14.5 us -> none  [local_part(): picked = lax.psum(jnp.where(is_owned, local_pick, 0.0), 'tp')]
    pmax x1 -> x0, blocking collectives: 13.9 us -> none  [local_part(): row_max = lax.pmax(local_max, 'tp')]
    unnamed x3 -> x2, local copies, waits for them, and re-layouts: 0.01 us -> 2.32 us
    reduce_sum x2 -> x0, other arithmetic: 1.85 us -> none  [the longest x1 0.97 us: local_part(): mean_sq = jnp.mean(x_float * x_float, axis=-1, keepdims=True)]
    reshape x0 -> x1, local copies, waits for them, and re-layouts: none -> 1.28 us  [local_part(): norm_w.reshape(1, depth)]
where the time goes in v1:
time: 48.2 us; the launch traced here: 48.1 us
  Pallas kernels  43.8 us (91%)
  local copies, waits for them, and re-layouts  3.59 us (7%)
  between operations  0.64 us (1%)
    pallas_call x1, Pallas kernels, local_part(): pl.pallas_call(functools.partial(head_kernel, group, tp, rows), out_shape...  43.8 us
    unnamed x2, local copies, waits for them, and re-layouts  2.32 us
    reshape x1, local copies, waits for them, and re-layouts, local_part(): norm_w.reshape(1, depth)  1.28 us

profile of v1, /device:TPU:81, one launch (start us, length us, event | category | flops | bytes accessed | tf_op | source)
XLA Modules:
  0.0 48.1 jit_solution(568449475385927867)
XLA Ops:
  0.6 1.3 %reshape.7.w_hbm = bf16[1,2048]{1,0:T(2,128)(2,1)} reshape(bf16[2048]{0:T(1024)(128)(2,1)} %param.5) | data formatting | bytes 8192 | tf_op jit(solution)/shard_map/reshape | solution.py:240
  1.9 43.8 %shard_map.59 = (f32[1,16]{1,0:T(1,128)}, f32[1,16]{1,0:T(1,128)}) custom-call(bf16[1,16,2048]{2,1,0:T(8,128)(2,1)} %hid_hbm.1, bf16[1,2048]{1,0:T(2,128)(2,1)} %reshape.7.w_hbm, bf16[32000,2048]{1,0:T(8,128)(2,1)} %emb_hbm.1, s32[1,16]{1,0:T(1,128)} %ids_hbm.1), custom_call_target="tpu_custom_call" | custom-call | tf_op jit(solution)/shard_map/pallas_call | solution.py:218
  45.8 1.1 %copy.8 = f32[1,16]{1,0:T(1,128)} copy(f32[1,16]{1,0:T(1,128)} %get-tuple-element.4) | data formatting | bytes 128
  46.9 1.2 %copy.9 = f32[1,16]{1,0:T(1,128)} copy(f32[1,16]{1,0:T(1,128)} %get-tuple-element.5) | data formatting | bytes 128

commit v2 on v1

--- a/solution.py
+++ b/solution.py
@@ -13,10 +13,11 @@
 HALVES = 2
 SHARE = 4
 CHUNK_ROWS = 800
+PARTS = 2
 
 
 def head_kernel(
-    group, tp, rows, hid_hbm, w_hbm, emb_hbm, ids_hbm, lp_ref, ent_ref,
+    group, tp, rows, hid_hbm, w_hbm, emb_hbm, ids_hbm, got_ref,
     hid_v, w_v, ids_v, hx, ids_x, hb, ebuf, zs, sbuf, rbuf,
     in_sem, esem, h_send, h_recv, f_send, f_recv, id_send, id_recv, s_send, s_recv,
 ):
@@ -51,7 +52,7 @@
             col = half * (c if o == 0 else 1 - c)
             copy = pltpu.make_async_copy(
                 emb_hbm.at[pl.ds(q * rows + j * chunk, chunk), pl.ds(pl.multiple_of(col, half), half)],
-                ebuf.at[o, pl.ds(j * chunk, chunk)],
+                ebuf.at[pl.ds(j * chunk, chunk), pl.ds(o * half, half)],
                 esem.at[j, o],
             )
             copy.start()
@@ -70,7 +71,7 @@
         copy.wait()
     x = hid_v[...].astype(jnp.float32)
     scale = lax.rsqrt(jnp.mean(x * x, axis=-1, keepdims=True) + EPS)
-    h = (x * scale * (1.0 + w_v[...].astype(jnp.float32))).astype(jnp.bfloat16)
+    h = (x * scale * (1.0 + w_v[...].astype(jnp.float32).reshape(1, depth))).astype(jnp.bfloat16)
     h32 = h.astype(jnp.float32)
     for s in range(HALVES):
         hx[q, s] = h32[:, s * half:(s + 1) * half]
@@ -94,7 +95,7 @@
 
     def place(p, o):
         col = c if o == 0 else 1 - c
-        hb[o, pl.ds(pl.multiple_of(p * npos, npos), npos), :] = hx[p, col].astype(jnp.bfloat16)
+        hb[pl.ds(pl.multiple_of(p * npos, npos), npos), o * half:(o + 1) * half] = hx[p, col].astype(jnp.bfloat16)
 
     for o in range(HALVES):
         place(q, o)
@@ -121,9 +122,19 @@
     first_row = tp_me * (rows * group) + q * rows
     want = want - first_row - lax.broadcasted_iota(jnp.int32, (8, LANES), 0)
 
-    def score(j, o):
-        return lax.dot_general(
-            ebuf[o, j * chunk:(j + 1) * chunk, :], hb[o], (((1,), (1,)), ((), ())), preferred_element_type=jnp.float32)
+    def score(j, lo, hi):
+        out = []
+        for m in range(PARTS):
+            first = j * chunk + m * (chunk // PARTS)
+            out.append(lax.dot_general(
+                ebuf[first:first + chunk // PARTS, lo:hi], hb[:, lo:hi], (((1,), (1,)), ((), ())),
+                preferred_element_type=jnp.float32))
+        return out
+
+    def keep(j, parts):
+        for m, part in enumerate(parts):
+            n = chunk // PARTS
+            zs[j % 2, m * n:(m + 1) * n, :group * npos] = part
 
     def stats(j, state):
         z = zs[j % 2].reshape(chunk // 8, 8, LANES)
@@ -148,15 +159,15 @@
     for j in range(nchunk):
         loads[j][0].wait()
         if j == 0:
-            first = score(0, 0)
+            first = score(0, 0, half)
             for r in range(1, group):
                 forward[r - 1].wait_recv()
                 place(lax.rem(q - r + group, group), 1)
             loads[0][1].wait()
-            zs[0, :, :group * npos] = first + score(0, 1)
+            keep(0, [u + v for u, v in zip(first, score(0, half, depth))])
         else:
             loads[j][1].wait()
-            zs[j % 2, :, :group * npos] = score(j, 0) + score(j, 1)
+            keep(j, score(j, 0, depth))
             state = stats(j - 1, state)
     state = stats(nchunk - 1, state)
 
@@ -192,7 +203,11 @@
     everyone.wait_recv()
     everyone.wait_send()
 
-    got = rbuf[...]
+    got_ref[...] = rbuf[...]
+
+
+def combine_kernel(npos, got_ref, lp_ref, ent_ref):
+    got = got_ref[...]
     values = pltpu.roll(got, LANES // 2, 2)
     top = jnp.max(got, axis=0)
     sums = jnp.sum(jnp.exp(got - top[None]) * values, axis=0)
@@ -215,19 +230,19 @@
         nchunk = rows // CHUNK_ROWS
         any_spec = pl.BlockSpec(memory_space=pl.ANY)
         dma = pltpu.SemaphoreType.DMA
-        return pl.pallas_call(
+        got = pl.pallas_call(
             functools.partial(head_kernel, group, tp, rows),
-            out_shape=[jax.ShapeDtypeStruct((1, npos), jnp.float32)] * 2,
+            out_shape=jax.ShapeDtypeStruct((group * tp, 1, LANES), jnp.float32),
             in_specs=[any_spec] * 4,
-            out_specs=[pl.BlockSpec(memory_space=pltpu.VMEM)] * 2,
+            out_specs=pl.BlockSpec(memory_space=pltpu.VMEM),
             scratch_shapes=[
                 pltpu.VMEM((npos, depth), jnp.bfloat16),
-                pltpu.VMEM((1, depth), jnp.bfloat16),
+                pltpu.VMEM((depth,), jnp.bfloat16),
                 pltpu.VMEM((1, npos), jnp.int32),
                 pltpu.VMEM((group, HALVES, npos, half), jnp.float32),
                 pltpu.VMEM((group, 1, LANES), jnp.int32),
-                pltpu.VMEM((HALVES, group * npos, half), jnp.bfloat16),
-                pltpu.VMEM((HALVES, rows, half), jnp.bfloat16),
+                pltpu.VMEM((group * npos, depth), jnp.bfloat16),
+                pltpu.VMEM((rows, depth), jnp.bfloat16),
                 pltpu.VMEM((2, CHUNK_ROWS, LANES), jnp.float32),
                 pltpu.VMEM((group, 1, LANES), jnp.float32),
                 pltpu.VMEM((group * tp, 1, LANES), jnp.float32),
@@ -237,7 +252,13 @@
             ],
             compiler_params=pltpu.CompilerParams(
                 collective_id=0, has_side_effects=True, vmem_limit_bytes=60 * 2**20),
-        )(hidden, norm_w.reshape(1, depth), embedding, draft_ids)
+        )(hidden, norm_w, embedding, draft_ids)
+        return pl.pallas_call(
+            functools.partial(combine_kernel, npos),
+            out_shape=[jax.ShapeDtypeStruct((1, npos), jnp.float32)] * 2,
+            in_specs=[pl.BlockSpec(memory_space=pltpu.VMEM)],
+            out_specs=[pl.BlockSpec(memory_space=pltpu.VMEM)] * 2,
+        )(got)
 
     return jax.shard_map(
         local_part, mesh=mesh,

time: 48.2 us -> 37.9 us (0.79)
  Pallas kernels: 43.8 us -> 37.1 us
  local copies, waits for them, and re-layouts: 3.59 us -> 0 us
    pallas_call x1, Pallas kernels: 43.8 us -> 35.7 us  [local_part(): pl.pallas_call(functools.partial(head_kernel, group, tp, rows), out_shape...]
    unnamed x2 -> x0, local copies, waits for them, and re-layouts: 2.32 us -> none
    pallas_call x0 -> x1, Pallas kernels: none -> 1.41 us  [local_part(): pl.pallas_call(functools.partial(combine_kernel, npos), out_shape=[jax.Sh...]
    reshape x1 -> x0, local copies, waits for them, and re-layouts: 1.28 us -> none  [local_part(): norm_w.reshape(1, depth)]
where the time goes in v2:
time: 37.9 us; the launch traced here: 37.7 us
  Pallas kernels  37.1 us (98%)
  between operations  0.64 us (2%)
    pallas_call x1, Pallas kernels, local_part(): pl.pallas_call(functools.partial(head_kernel, group, tp, rows), out_shape...  35.7 us
    pallas_call x1, Pallas kernels, local_part(): pl.pallas_call(functools.partial(combine_kernel, npos), out_shape=[jax.Sh...  1.41 us

profile of v2, /device:TPU:81, one launch (start us, length us, event | category | flops | bytes accessed | tf_op | source)
XLA Modules:
  0.0 37.7 jit_solution(6335916812946913707)
XLA Ops:
  0.6 35.7 %shard_map.59.got_ref = f32[32,1,128]{2,1,0:T(1,128)} custom-call(bf16[1,16,2048]{2,1,0:T(8,128)(2,1)} %hid_hbm.1, bf16[2048]{0:T(1024)(128)(2,1)} %w_hbm.1, bf16[32000,2048]{1,0:T(8,128)(2,1)} %emb_hbm.1, s32[1,16]{1,0:T(1,128)} %ids_hbm.1), custom_call_target="tpu_custom_call" | custom-call | tf_op jit(solution)/shard_map/pallas_call | solution.py:233
  36.3 1.4 %shard_map.60 = (f32[1,16]{1,0:T(1,128)}, f32[1,16]{1,0:T(1,128)}) custom-call(f32[32,1,128]{2,1,0:T(1,128)} %shard_map.59.got_ref), custom_call_target="tpu_custom_call" | custom-call | tf_op jit(solution)/shard_map/pallas_call | solution.py:256

commit v3 on v2

--- a/solution.py
+++ b/solution.py
@@ -14,6 +14,9 @@
 SHARE = 4
 CHUNK_ROWS = 800
 PARTS = 2
+BEFORE_BARRIER = 2
+BEFORE_FORWARD = 5
+BLOCKS = (4, 99)
 
 
 def head_kernel(
@@ -47,17 +50,23 @@
         copy.start()
     loads = []
     for j in range(nchunk):
-        pair = []
         for o in range(HALVES):
             col = half * (c if o == 0 else 1 - c)
-            copy = pltpu.make_async_copy(
+            loads.append(pltpu.make_async_copy(
                 emb_hbm.at[pl.ds(q * rows + j * chunk, chunk), pl.ds(pl.multiple_of(col, half), half)],
                 ebuf.at[pl.ds(j * chunk, chunk), pl.ds(o * half, half)],
                 esem.at[j, o],
-            )
+            ))
+
+    def fetch(lo, hi):
+        for copy in loads[lo * HALVES:hi * HALVES]:
             copy.start()
-            pair.append(copy)
-        loads.append(pair)
+
+    def arrive(lo, hi):
+        for copy in loads[lo * HALVES:hi * HALVES]:
+            copy.wait()
+
+    fetch(0, BEFORE_BARRIER)
 
     barrier = pltpu.get_barrier_semaphore()
     for r in range(group):
@@ -77,6 +86,7 @@
         hx[q, s] = h32[:, s * half:(s + 1) * half]
     ids_x[q] = jnp.concatenate([ids_v[...], jnp.full((1, LANES - npos), -1, jnp.int32)], axis=1)
 
+    zs[:, :, group * npos:] = jnp.zeros((nchunk, chunk, LANES - group * npos), jnp.float32)
     pl.semaphore_wait(barrier, nsrc - 1)
 
     direct, ident = [], []
@@ -92,6 +102,7 @@
             device_id=(peer(r), tp_me), device_id_type=MESH)
         copy.start()
         ident.append(copy)
+    fetch(BEFORE_BARRIER, BEFORE_FORWARD)
 
     def place(p, o):
         col = c if o == 0 else 1 - c
@@ -109,6 +120,7 @@
         copy.start()
         forward.append(copy)
         place(p, 0)
+    fetch(BEFORE_FORWARD, nchunk)
     for copy in ident:
         copy.wait_recv()
 
@@ -134,10 +146,10 @@
     def keep(j, parts):
         for m, part in enumerate(parts):
             n = chunk // PARTS
-            zs[j % 2, m * n:(m + 1) * n, :group * npos] = part
+            zs[j, m * n:(m + 1) * n, :group * npos] = part
 
     def stats(j, state):
-        z = zs[j % 2].reshape(chunk // 8, 8, LANES)
+        z = zs[j].reshape(chunk // 8, 8, LANES)
         top = jnp.max(z, axis=0)
         row = lax.broadcasted_iota(jnp.int32, (chunk // 8, 8, LANES), 0) * 8 + j * chunk
         pick = jnp.sum(jnp.where(row == want[None], z, 0.0), axis=0)
@@ -153,22 +165,22 @@
             pick = pick + state[3]
         return top, total, weighted, pick
 
-    for s in range(2):
-        zs[s] = jnp.zeros((chunk, LANES), jnp.float32)
+    loads[0].wait()
+    first = score(0, 0, half)
+    for r in range(1, group):
+        forward[r - 1].wait_recv()
+        place(lax.rem(q - r + group, group), 1)
+    loads[1].wait()
+    keep(0, [u + v for u, v in zip(first, score(0, half, depth))])
     state = None
-    for j in range(nchunk):
-        loads[j][0].wait()
-        if j == 0:
-            first = score(0, 0, half)
-            for r in range(1, group):
-                forward[r - 1].wait_recv()
-                place(lax.rem(q - r + group, group), 1)
-            loads[0][1].wait()
-            keep(0, [u + v for u, v in zip(first, score(0, half, depth))])
-        else:
-            loads[j][1].wait()
+    at = 1
+    for size in BLOCKS:
+        end = min(at + size, nchunk)
+        arrive(at, end)
+        for j in range(at, end):
             keep(j, score(j, 0, depth))
             state = stats(j - 1, state)
+        at = end
     state = stats(nchunk - 1, state)
 
     top8, total8, weighted8, pick8 = state
@@ -243,7 +255,7 @@
                 pltpu.VMEM((group, 1, LANES), jnp.int32),
                 pltpu.VMEM((group * npos, depth), jnp.bfloat16),
                 pltpu.VMEM((rows, depth), jnp.bfloat16),
-                pltpu.VMEM((2, CHUNK_ROWS, LANES), jnp.float32),
+                pltpu.VMEM((nchunk, CHUNK_ROWS, LANES), jnp.float32),
                 pltpu.VMEM((group, 1, LANES), jnp.float32),
                 pltpu.VMEM((group * tp, 1, LANES), jnp.float32),
                 dma((3,)), dma((nchunk, HALVES)),

time: 37.9 us -> 31.4 us (0.83)
  Pallas kernels: 37.1 us -> 30.6 us
    pallas_call x1, Pallas kernels: 35.7 us -> 29.2 us  [local_part(): pl.pallas_call(functools.partial(head_kernel, group, tp, rows), out_shape...]
where the time goes in v3:
time: 31.4 us; the launch traced here: 31.2 us
  Pallas kernels  30.6 us (97%)
  between operations  0.64 us (2%)
    pallas_call x1, Pallas kernels, local_part(): pl.pallas_call(functools.partial(head_kernel, group, tp, rows), out_shape...  29.2 us
    pallas_call x1, Pallas kernels, local_part(): pl.pallas_call(functools.partial(combine_kernel, npos), out_shape=[jax.Sh...  1.41 us

profile of v3, /device:TPU:81, one launch (start us, length us, event | category | flops | bytes accessed | tf_op | source)
XLA Modules:
  0.0 31.2 jit_solution(2151659925178903313)
XLA Ops:
  0.6 29.2 %shard_map.59.got_ref = f32[32,1,128]{2,1,0:T(1,128)} custom-call(bf16[1,16,2048]{2,1,0:T(8,128)(2,1)} %hid_hbm.1, bf16[2048]{0:T(1024)(128)(2,1)} %w_hbm.1, bf16[32000,2048]{1,0:T(8,128)(2,1)} %emb_hbm.1, s32[1,16]{1,0:T(1,128)} %ids_hbm.1), custom_call_target="tpu_custom_call" | custom-call | tf_op jit(solution)/shard_map/pallas_call | solution.py:245
  29.8 1.4 %shard_map.60 = (f32[1,16]{1,0:T(1,128)}, f32[1,16]{1,0:T(1,128)}) custom-call(f32[32,1,128]{2,1,0:T(1,128)} %shard_map.59.got_ref), custom_call_target="tpu_custom_call" | custom-call | tf_op jit(solution)/shard_map/pallas_call | solution.py:268

commit v4 on v2

v4 whole, which is shorter than its diff:
```python
import functools

import jax
import jax.numpy as jnp
from jax import lax
from jax.experimental import pallas as pl
from jax.experimental.pallas import tpu as pltpu
from jax.sharding import PartitionSpec as P

EPS = 1e-6
MESH = pl.DeviceIdType.MESH
LANES = 128
HALVES = 2
PARTS = 2
SHARE = 4
OWN = (1024, 1024, 1024, 1024)
OWN_BEFORE = 3
CHUNK = 1024
BLOCKS = (1, 1, 1, 1, 1, 1, 1, 1)
FIRST_LOADS = 1
SECOND_LOADS = 5


def shared_chunks(rows):
    sizes = [CHUNK] * (rows // CHUNK)
    return sizes + ([rows % CHUNK] if rows % CHUNK else [])


def dot_rows(e, h):
    n = e.shape[0] // PARTS
    return [
        lax.dot_general(e[m * n:(m + 1) * n, :], h[...], (((1,), (1,)), ((), ())), preferred_element_type=jnp.float32)
        for m in range(PARTS)
    ]


def fold(z, first, want, state):
    n, width = z.shape
    z = z.reshape(n // 8, 8, width)
    row = lax.broadcasted_iota(jnp.int32, z.shape, 0) * 8 + first
    pick = jnp.sum(jnp.where(row == want[None], z, 0.0), axis=0)
    top = jnp.max(z, axis=0)
    if state is not None:
        top = jnp.maximum(top, state[0])
    e = jnp.exp(z - top[None])
    total = jnp.sum(e, axis=0)
    weighted = jnp.sum(e * z, axis=0)
    if state is not None:
        fade = jnp.exp(state[0] - top)
        total, weighted, pick = total + state[1] * fade, weighted + state[2] * fade, pick + state[3]
    return top, total, weighted, pick


def head_kernel(
    group, tp, hid_hbm, w_hbm, emb_hbm, ids_hbm, got_ref,
    hid_v, w_v, ids_v, hx, ids_x, h_own, h_all, ebuf, zo, zs, sbuf, rbuf,
    in_sem, esem, h_send, h_recv, f_send, f_recv, id_send, id_recv, s_send, s_recv,
):
    npos, depth = hid_v.shape
    half = depth // HALVES
    shard = emb_hbm.shape[0]
    n_own = sum(OWN)
    rows = (shard - n_own) // group
    shared = shared_chunks(rows)
    nsrc = group * tp
    width = group * npos

    dp_me = lax.axis_index("dp")
    tp_me = lax.axis_index("tp")
    q = lax.rem(dp_me, group)
    base = dp_me - q
    c = lax.rem(tp_me, 2)
    sibling = tp_me + 1 - 2 * c
    me = q * tp + tp_me

    def member(r):
        if group == 4:
            a, b = q // 2, lax.rem(q, 2)
            return lax.rem(a + r // 2, 2) * 2 + lax.rem(b + r % 2, 2)
        return lax.rem(q + r, group)

    others = tuple(range(group - 1, 0, -1))

    small = [
        pltpu.make_async_copy(hid_hbm.at[0], hid_v, in_sem.at[0]),
        pltpu.make_async_copy(w_hbm, w_v, in_sem.at[1]),
        pltpu.make_async_copy(ids_hbm, ids_v, in_sem.at[2]),
    ]
    for copy in small:
        copy.start()
    loads, spans, at = [], [], 0
    for j, n in enumerate(OWN + tuple(shared)):
        src = at if j < len(OWN) else at + q * rows
        loads.append(pltpu.make_async_copy(
            emb_hbm.at[pl.ds(src, n)], ebuf.at[pl.ds(at, n)], esem.at[j]))
        spans.append((at, n))
        at += n

    for copy in loads[:FIRST_LOADS]:
        copy.start()

    barrier = pltpu.get_barrier_semaphore()
    far_first = (tp // 2, tp // 2 + 1) + tuple(t for t in range(tp) if t not in (tp // 2, tp // 2 + 1))
    for r in others + (0,):
        for t in far_first:
            if r or t:
                pl.semaphore_signal(
                    barrier, inc=1, device_id=(base + member(r), lax.rem(tp_me + t, tp)), device_id_type=MESH)

    small[0].wait()
    small[1].wait()
    x = hid_v[...].astype(jnp.float32)
    scale = lax.rsqrt(jnp.mean(x * x, axis=-1, keepdims=True) + EPS)
    h = (x * scale * (1.0 + w_v[...].astype(jnp.float32).reshape(1, depth))).astype(jnp.bfloat16)
    h32 = h.astype(jnp.float32)
    for s in range(HALVES):
        hx[q, s] = h32[:, s * half:(s + 1) * half]
    h_own[...] = h
    small[2].wait()
    ids_x[q] = jnp.concatenate([ids_v[...], jnp.full((1, LANES - npos), -1, jnp.int32)], axis=1)

    pl.semaphore_wait(barrier, nsrc - 1)

    direct, ident, forward = {}, {}, {}
    for r in others:
        direct[r] = pltpu.make_async_remote_copy(
            src_ref=hx.at[q, c], dst_ref=hx.at[q, c], send_sem=h_send.at[r], recv_sem=h_recv.at[r],
            device_id=(base + member(r), tp_me), device_id_type=MESH)
        direct[r].start()
    for r in others:
        ident[r] = pltpu.make_async_remote_copy(
            src_ref=ids_x.at[q], dst_ref=ids_x.at[q], send_sem=id_send.at[r], recv_sem=id_recv.at[r],
            device_id=(base + member(r), tp_me), device_id_type=MESH)
        ident[r].start()
    for copy in loads[FIRST_LOADS:SECOND_LOADS]:
        copy.start()

    def place(p, s):
        h_all[s, pl.ds(pl.multiple_of(p * npos, npos), npos), :] = hx[p, s].astype(jnp.bfloat16)

    sub = lax.broadcasted_iota(jnp.int32, (8, npos), 0)
    want_own = jnp.broadcast_to(ids_x[q][:, :npos], (8, npos)) - tp_me * shard - sub
    own = None

    def own_fold(j, own):
        lo, n = spans[j]
        return fold(zo[j, :n, :], lo, want_own, own)

    def own_chunk(j, own):
        lo, n = spans[j]
        loads[j].wait()
        for m, part in enumerate(dot_rows(ebuf.at[pl.ds(lo, n)], h_own)):
            zo[j, m * (n // PARTS):(m + 1) * (n // PARTS), :] = part
        return own_fold(j - 1, own) if j else own

    for j in range(OWN_BEFORE):
        own = own_chunk(j, own)

    for r in others:
        p = member(r)
        direct[r].wait_recv()
        forward[r] = pltpu.make_async_remote_copy(
            src_ref=hx.at[p, c], dst_ref=hx.at[p, c], send_sem=f_send.at[r], recv_sem=f_recv.at[r],
            device_id=(dp_me, sibling), device_id_type=MESH)
        forward[r].start()
    for copy in loads[SECOND_LOADS:]:
        copy.start()
    for r in others:
        ident[r].wait_recv()
        place(member(r), c)
    for s in range(HALVES):
        place(q, s)

    lane = lax.broadcasted_iota(jnp.int32, (8, LANES), 1)
    want = jnp.full((8, LANES), -1, jnp.int32)
    for p in range(group):
        moved = jnp.broadcast_to(ids_x[p], (8, LANES))
        if p:
            moved = pltpu.roll(moved, p * npos, 1)
        want = jnp.where((lane >= p * npos) & (lane < (p + 1) * npos), moved, want)
    first_row = tp_me * shard + n_own + q * rows
    want = (want - first_row - lax.broadcasted_iota(jnp.int32, (8, LANES), 0))[:, :width]

    for j in range(OWN_BEFORE, len(OWN)):
        own = own_chunk(j, own)
    own = own_fold(len(OWN) - 1, own)

    mine = (lane >= q * npos) & (lane < (q + 1) * npos)

    def spread(v, other):
        v = jnp.concatenate([v, jnp.zeros((8, LANES - npos), jnp.float32)], axis=1)
        return jnp.where(mine, pltpu.roll(v, q * npos, 1), other)[:, :width]

    state = tuple(spread(v, other) for v, other in zip(own, (-jnp.inf, 0.0, 0.0, 0.0)))

    for r in others:
        forward[r].wait_recv()
        place(member(r), 1 - c)

    h_pos = jnp.concatenate([h_all[s] for s in range(HALVES)], axis=1)
    n_chunks = len(shared)
    at = 0
    for size in BLOCKS:
        end = min(at + size, n_chunks)
        for j in range(at, end):
            loads[len(OWN) + j].wait()
        for j in range(at, end):
            lo, n = spans[len(OWN) + j]
            for m, part in enumerate(dot_rows(ebuf.at[pl.ds(lo, n)], h_pos)):
                zs[j, m * (n // PARTS):(m + 1) * (n // PARTS), :] = part
            if j:
                before, count = spans[len(OWN) + j - 1]
                state = fold(zs[j - 1, :count, :], before - n_own, want, state)
        at = end
    lo, n = spans[-1]
    state = fold(zs[n_chunks - 1, :n, :], lo - n_own, want, state)

    top8, total8, weighted8, pick8 = (
        jnp.concatenate([v, jnp.zeros((8, LANES - width), jnp.float32)], axis=1) for v in state)
    top = jnp.max(top8, axis=0, keepdims=True)
    fade = jnp.exp(top8 - top)
    full = lambda v: jnp.broadcast_to(v, (8, LANES))
    top = full(top)
    total = full(jnp.sum(total8 * fade, axis=0, keepdims=True))
    weighted = full(jnp.sum(weighted8 * fade, axis=0, keepdims=True))
    pick = full(jnp.sum(pick8, axis=0, keepdims=True))
    for p in range(group):
        message = jnp.zeros((8, LANES), jnp.float32)
        for at, v in ((0, top), (1, top), (4, total), (5, weighted), (6, pick)):
            shift = (at * npos - p * npos) % LANES
            moved = pltpu.roll(v, shift, 1) if shift else v
            message = jnp.where((lane >= at * npos) & (lane < (at + 1) * npos), moved, message)
        sbuf[p] = message[:1]

    for r in others + (0,):
        for t in far_first:
            if r or t:
                pltpu.make_async_remote_copy(
                    src_ref=sbuf.at[member(r)], dst_ref=rbuf.at[me], send_sem=s_send, recv_sem=s_recv,
                    device_id=(base + member(r), lax.rem(tp_me + t, tp)), device_id_type=MESH).start()
    rbuf[me] = sbuf[q]
    for copies in (direct, ident, forward):
        for copy in copies.values():
            copy.wait_send()
    everyone = pltpu.make_async_remote_copy(
        src_ref=rbuf.at[pl.ds(0, nsrc - 1)], dst_ref=rbuf.at[pl.ds(0, nsrc - 1)], send_sem=s_send, recv_sem=s_recv,
        device_id=(dp_me, tp_me), device_id_type=MESH)
    everyone.wait_recv()
    everyone.wait_send()
    got_ref[...] = rbuf[...]


def combine_kernel(npos, got_ref, lp_ref, ent_ref):
    got = got_ref[...]
    values = pltpu.roll(got, LANES // 2, 2)
    top = jnp.max(got, axis=0)
    sums = jnp.sum(jnp.exp(got - top[None]) * values, axis=0)
    total = sums[:, :npos]
    weighted = pltpu.roll(sums, LANES - npos, 1)[:, :npos]
    pick = pltpu.roll(sums, LANES - 2 * npos, 1)[:, :npos]
    log_norm = top[:, :npos] + jnp.log(total)
    lp_ref[...] = pick - log_norm
    ent_ref[...] = log_norm - weighted / total


def solution(mesh):
    tp = mesh.shape["tp"]
    group = next(n for n in (SHARE, 2, 1) if mesh.shape["dp"] % n == 0)

    def local_part(hidden, norm_w, embedding, draft_ids):
        npos, depth = hidden.shape[1:]
        shard = embedding.shape[0]
        rows = (shard - sum(OWN)) // group
        half = depth // HALVES
        n_shared = len(shared_chunks(rows))
        any_spec = pl.BlockSpec(memory_space=pl.ANY)
        dma = pltpu.SemaphoreType.DMA
        got = pl.pallas_call(
            functools.partial(head_kernel, group, tp),
            out_shape=pltpu.VMEM((group * tp, 1, LANES), jnp.float32),
            in_specs=[any_spec] * 4,
            out_specs=pl.BlockSpec(memory_space=pltpu.VMEM),
            scratch_shapes=[
                pltpu.VMEM((npos, depth), jnp.bfloat16),
                pltpu.VMEM((depth,), jnp.bfloat16),
                pltpu.VMEM((1, npos), jnp.int32),
                pltpu.VMEM((group, HALVES, npos, half), jnp.float32),
                pltpu.VMEM((group, 1, LANES), jnp.int32),
                pltpu.VMEM((npos, depth), jnp.bfloat16),
                pltpu.VMEM((HALVES, group * npos, half), jnp.bfloat16),
                pltpu.VMEM((sum(OWN) + rows, depth), jnp.bfloat16),
                pltpu.VMEM((len(OWN), max(OWN), npos), jnp.float32),
                pltpu.VMEM((n_shared, CHUNK, group * npos), jnp.float32),
                pltpu.VMEM((group, 1, LANES), jnp.float32),
                pltpu.VMEM((group * tp, 1, LANES), jnp.float32),
                dma((3,)), dma((len(OWN) + n_shared,)),
                dma((group,)), dma((group,)), dma((group,)), dma((group,)), dma((group,)), dma((group,)),
                dma, dma,
            ],
            compiler_params=pltpu.CompilerParams(
                collective_id=0, has_side_effects=True, vmem_limit_bytes=60 * 2**20),
        )(hidden, norm_w, embedding, draft_ids)
        return pl.pallas_call(
            functools.partial(combine_kernel, npos),
            out_shape=[jax.ShapeDtypeStruct((1, npos), jnp.float32)] * 2,
            in_specs=[pl.BlockSpec(memory_space=pltpu.VMEM)],
            out_specs=[pl.BlockSpec(memory_space=pltpu.VMEM)] * 2,
            compiler_params=pltpu.CompilerParams(vmem_limit_bytes=2**20),
        )(got)

    return jax.shard_map(
        local_part, mesh=mesh,
        in_specs=(P("dp", None, None), P(None), P("tp", None), P("dp", None)),
        out_specs=(P("dp", None), P("dp", None)), check_vma=False)
```

time: 37.9 us -> 29.7 us (0.78)
  Pallas kernels: 37.1 us -> 29 us
    pallas_call x1, Pallas kernels: 35.7 us -> 28.3 us  [local_part(): pl.pallas_call(functools.partial(head_kernel, group, tp), out_shape=pltpu...]
    pallas_call x1, Pallas kernels: 1.41 us -> 0.69 us  [local_part(): pl.pallas_call(functools.partial(combine_kernel, npos), out_shape=[jax.Sh...]
where the time goes in v4:
time: 29.7 us; the launch traced here: 29.6 us
  Pallas kernels  29 us (98%)
  between operations  0.64 us (2%)
    pallas_call x1, Pallas kernels, local_part(): pl.pallas_call(functools.partial(head_kernel, group, tp), out_shape=pltpu...  28.3 us
    pallas_call x1, Pallas kernels, local_part(): pl.pallas_call(functools.partial(combine_kernel, npos), out_shape=[jax.Sh...  0.69 us

profile of v4, /device:TPU:81, one launch (start us, length us, event | category | flops | bytes accessed | tf_op | source)
XLA Modules:
  0.0 29.6 jit_solution(6264390446552073765)
XLA Ops:
  0.6 28.3 %shard_map.59.got_ref = f32[32,1,128]{2,1,0:T(1,128)S(1)} custom-call(bf16[1,16,2048]{2,1,0:T(8,128)(2,1)} %hid_hbm.1, bf16[2048]{0:T(1024)(128)(2,1)} %w_hbm.1, bf16[32000,2048]{1,0:T(8,128)(2,1)} %emb_hbm.1, s32[1,16]{1,0:T(1,128)} %ids_hbm.1), custom_call_target="tpu_custom_call" | custom-call | tf_op jit(solution)/shard_map/pallas_call | solution.py:278
  28.9 0.7 %shard_map.60 = (f32[1,16]{1,0:T(1,128)}, f32[1,16]{1,0:T(1,128)}) custom-call(f32[32,1,128]{2,1,0:T(1,128)S(1)} %shard_map.59.got_ref), custom_call_target="tpu_custom_call" | custom-call | tf_op jit(solution)/shard_map/pallas_call | solution.py:303

commit v5 on v4

--- a/solution.py
+++ b/solution.py
@@ -16,7 +16,7 @@
 OWN = (1024, 1024, 1024, 1024)
 OWN_BEFORE = 3
 CHUNK = 1024
-BLOCKS = (1, 1, 1, 1, 1, 1, 1, 1)
+BLOCKS = (1, 2, 2, 2)
 FIRST_LOADS = 1
 SECOND_LOADS = 5
 
@@ -54,7 +54,7 @@
 def head_kernel(
     group, tp, hid_hbm, w_hbm, emb_hbm, ids_hbm, got_ref,
     hid_v, w_v, ids_v, hx, ids_x, h_own, h_all, ebuf, zo, zs, sbuf, rbuf,
-    in_sem, esem, h_send, h_recv, f_send, f_recv, id_send, id_recv, s_send, s_recv,
+    in_sem, esem, h_send, h_recv, f_send, f_recv, id_send, id_recv, s_send, s_recv, token,
 ):
     npos, depth = hid_v.shape
     half = depth // HALVES
@@ -100,12 +100,10 @@
         copy.start()
 
     barrier = pltpu.get_barrier_semaphore()
-    far_first = (tp // 2, tp // 2 + 1) + tuple(t for t in range(tp) if t not in (tp // 2, tp // 2 + 1))
-    for r in others + (0,):
-        for t in far_first:
-            if r or t:
-                pl.semaphore_signal(
-                    barrier, inc=1, device_id=(base + member(r), lax.rem(tp_me + t, tp)), device_id_type=MESH)
+    beside = (lax.rem(tp_me + 2, tp), lax.rem(tp_me + tp - 2, tp))
+    near = [(base + member(r), tp_me) for r in others] + [(dp_me, sibling)] + [(dp_me, t) for t in beside]
+    for device in near:
+        pl.semaphore_signal(barrier, inc=1, device_id=device, device_id_type=MESH)
 
     small[0].wait()
     small[1].wait()
@@ -119,7 +117,7 @@
     small[2].wait()
     ids_x[q] = jnp.concatenate([ids_v[...], jnp.full((1, LANES - npos), -1, jnp.int32)], axis=1)
 
-    pl.semaphore_wait(barrier, nsrc - 1)
+    pl.semaphore_wait(barrier, len(near))
 
     direct, ident, forward = {}, {}, {}
     for r in others:
@@ -135,6 +133,15 @@
     for copy in loads[FIRST_LOADS:SECOND_LOADS]:
         copy.start()
 
+    def tell(k):
+        for device in near[-2:] if k < 2 else near[-3:-2]:
+            pl.semaphore_signal(token.at[k], inc=1, device_id=device, device_id_type=MESH)
+
+    def hear(k):
+        pl.semaphore_wait(token.at[k], 2 if k < 2 else 1)
+
+    tell(0)
+
     def place(p, s):
         h_all[s, pl.ds(pl.multiple_of(p * npos, npos), npos), :] = hx[p, s].astype(jnp.bfloat16)
 
@@ -155,6 +162,9 @@
 
     for j in range(OWN_BEFORE):
         own = own_chunk(j, own)
+        if j == 1:
+            hear(0)
+            tell(1)
 
     for r in others:
         p = member(r)
@@ -165,6 +175,8 @@
         forward[r].start()
     for copy in loads[SECOND_LOADS:]:
         copy.start()
+    hear(1)
+    tell(2)
     for r in others:
         ident[r].wait_recv()
         place(member(r), c)
@@ -196,6 +208,8 @@
     for r in others:
         forward[r].wait_recv()
         place(member(r), 1 - c)
+
+    hear(2)
 
     h_pos = jnp.concatenate([h_all[s] for s in range(HALVES)], axis=1)
     n_chunks = len(shared)
@@ -232,6 +246,7 @@
             message = jnp.where((lane >= at * npos) & (lane < (at + 1) * npos), moved, message)
         sbuf[p] = message[:1]
 
+    far_first = (tp // 2, tp // 2 + 1) + tuple(t for t in range(tp) if t not in (tp // 2, tp // 2 + 1))
     for r in others + (0,):
         for t in far_first:
             if r or t:
@@ -295,7 +310,7 @@
                 pltpu.VMEM((group * tp, 1, LANES), jnp.float32),
                 dma((3,)), dma((len(OWN) + n_shared,)),
                 dma((group,)), dma((group,)), dma((group,)), dma((group,)), dma((group,)), dma((group,)),
-                dma, dma,
+                dma, dma, pltpu.SemaphoreType.REGULAR((3,)),
             ],
             compiler_params=pltpu.CompilerParams(
                 collective_id=0, has_side_effects=True, vmem_limit_bytes=60 * 2**20),

time: 29.7 us -> 29.2 us (0.983)
  Pallas kernels: 29 us -> 28.5 us
    pallas_call x1, Pallas kernels: 28.3 us -> 27.8 us  [local_part(): pl.pallas_call(functools.partial(head_kernel, group, tp), out_shape=pltpu...]
where the time goes in v5:
time: 29.2 us
  Pallas kernels  28.5 us (98%)
  between operations  0.64 us (2%)
    pallas_call x1, Pallas kernels, local_part(): pl.pallas_call(functools.partial(head_kernel, group, tp), out_shape=pltpu...  27.8 us
    pallas_call x1, Pallas kernels, local_part(): pl.pallas_call(functools.partial(combine_kernel, npos), out_shape=[jax.Sh...  0.69 us

profile of v5, /device:TPU:81, one launch (start us, length us, event | category | flops | bytes accessed | tf_op | source)
XLA Modules:
  0.0 29.2 jit_solution(16821919019810516746)
XLA Ops:
  0.6 27.8 %shard_map.59.got_ref = f32[32,1,128]{2,1,0:T(1,128)S(1)} custom-call(bf16[1,16,2048]{2,1,0:T(8,128)(2,1)} %hid_hbm.1, bf16[2048]{0:T(1024)(128)(2,1)} %w_hbm.1, bf16[32000,2048]{1,0:T(8,128)(2,1)} %emb_hbm.1, s32[1,16]{1,0:T(1,128)} %ids_hbm.1), custom_call_target="tpu_custom_call" | custom-call | tf_op jit(solution)/shard_map/pallas_call | solution.py:293
  28.5 0.7 %shard_map.60 = (f32[1,16]{1,0:T(1,128)}, f32[1,16]{1,0:T(1,128)}) custom-call(f32[32,1,128]{2,1,0:T(1,128)S(1)} %shard_map.59.got_ref), custom_call_target="tpu_custom_call" | custom-call | tf_op jit(solution)/shard_map/pallas_call | solution.py:318

commit v6 on v5

--- a/solution.py
+++ b/solution.py
@@ -13,12 +13,13 @@
 HALVES = 2
 PARTS = 2
 SHARE = 4
-OWN = (1024, 1024, 1024, 1024)
-OWN_BEFORE = 3
+OWN = (1280, 1280)
 CHUNK = 1024
-BLOCKS = (1, 2, 2, 2)
+UNIT = 512
+EARLY = 2
+BLOCKS = (1, 1, 1, 1, 2)
 FIRST_LOADS = 1
-SECOND_LOADS = 5
+SECOND_LOADS = 4
 
 
 def shared_chunks(rows):
@@ -29,7 +30,7 @@
 def dot_rows(e, h):
     n = e.shape[0] // PARTS
     return [
-        lax.dot_general(e[m * n:(m + 1) * n, :], h[...], (((1,), (1,)), ((), ())), preferred_element_type=jnp.float32)
+        lax.dot_general(e[m * n:(m + 1) * n, :], h, (((1,), (1,)), ((), ())), preferred_element_type=jnp.float32)
         for m in range(PARTS)
     ]
 
@@ -153,19 +154,17 @@
         lo, n = spans[j]
         return fold(zo[j, :n, :], lo, want_own, own)
 
-    def own_chunk(j, own):
+    h_mine = h_own[...]
+    for j in range(len(OWN)):
         lo, n = spans[j]
         loads[j].wait()
-        for m, part in enumerate(dot_rows(ebuf.at[pl.ds(lo, n)], h_own)):
+        for m, part in enumerate(dot_rows(ebuf.at[pl.ds(lo, n)], h_mine)):
             zo[j, m * (n // PARTS):(m + 1) * (n // PARTS), :] = part
-        return own_fold(j - 1, own) if j else own
-
-    for j in range(OWN_BEFORE):
-        own = own_chunk(j, own)
-        if j == 1:
+        if j:
+            own = own_fold(j - 1, own)
+        if j == 0:
             hear(0)
             tell(1)
-
     for r in others:
         p = member(r)
         direct[r].wait_recv()
@@ -193,9 +192,29 @@
     first_row = tp_me * shard + n_own + q * rows
     want = (want - first_row - lax.broadcasted_iota(jnp.int32, (8, LANES), 0))[:, :width]
 
-    for j in range(OWN_BEFORE, len(OWN)):
-        own = own_chunk(j, own)
-    own = own_fold(len(OWN) - 1, own)
+    units = []
+    for j in range(len(shared)):
+        lo, n = spans[len(OWN) + j]
+        units.append([(lo + u, min(UNIT, n - u)) for u in range(0, n, UNIT)])
+    order = [unit for chunk in units for unit in chunk]
+
+    def keep(unit, col, width_in, h, add):
+        lo, n = unit
+        for m, part in enumerate(dot_rows(ebuf.at[pl.ds(lo, n), pl.ds(col, width_in)], h)):
+            at = slice(m * (n // PARTS), (m + 1) * (n // PARTS))
+            u = order.index(unit)
+            zs[u, at, :] = part + zs[u, at, :] if add else part
+
+    def shared_fold(unit, state):
+        lo, n = unit
+        return fold(zs[order.index(unit), :n, :], lo - n_own, want, state)
+
+    for j in range(EARLY):
+        loads[len(OWN) + j].wait()
+        for unit in units[j]:
+            keep(unit, pl.multiple_of(c * half, half), half, h_all[c], False)
+        if j == 0:
+            own = own_fold(len(OWN) - 1, own)
 
     mine = (lane >= q * npos) & (lane < (q + 1) * npos)
 
@@ -208,26 +227,28 @@
     for r in others:
         forward[r].wait_recv()
         place(member(r), 1 - c)
-
     hear(2)
+    pending = None
+    for j in range(EARLY):
+        for unit in units[j]:
+            keep(unit, pl.multiple_of((1 - c) * half, half), half, h_all[1 - c], True)
+            if pending is not None:
+                state = shared_fold(pending, state)
+            pending = unit
 
     h_pos = jnp.concatenate([h_all[s] for s in range(HALVES)], axis=1)
-    n_chunks = len(shared)
-    at = 0
+    at = EARLY
     for size in BLOCKS:
-        end = min(at + size, n_chunks)
+        end = min(at + size, len(shared))
         for j in range(at, end):
             loads[len(OWN) + j].wait()
         for j in range(at, end):
-            lo, n = spans[len(OWN) + j]
-            for m, part in enumerate(dot_rows(ebuf.at[pl.ds(lo, n)], h_pos)):
-                zs[j, m * (n // PARTS):(m + 1) * (n // PARTS), :] = part
-            if j:
-                before, count = spans[len(OWN) + j - 1]
-                state = fold(zs[j - 1, :count, :], before - n_own, want, state)
+            for unit in units[j]:
+                keep(unit, 0, depth, h_pos, False)
+                state = shared_fold(pending, state)
+                pending = unit
         at = end
-    lo, n = spans[-1]
-    state = fold(zs[n_chunks - 1, :n, :], lo - n_own, want, state)
+    state = shared_fold(pending, state)
 
     top8, total8, weighted8, pick8 = (
         jnp.concatenate([v, jnp.zeros((8, LANES - width), jnp.float32)], axis=1) for v in state)
@@ -288,6 +309,7 @@
         rows = (shard - sum(OWN)) // group
         half = depth // HALVES
         n_shared = len(shared_chunks(rows))
+        n_units = sum(-(-n // UNIT) for n in shared_chunks(rows))
         any_spec = pl.BlockSpec(memory_space=pl.ANY)
         dma = pltpu.SemaphoreType.DMA
         got = pl.pallas_call(
@@ -305,7 +327,7 @@
                 pltpu.VMEM((HALVES, group * npos, half), jnp.bfloat16),
                 pltpu.VMEM((sum(OWN) + rows, depth), jnp.bfloat16),
                 pltpu.VMEM((len(OWN), max(OWN), npos), jnp.float32),
-                pltpu.VMEM((n_shared, CHUNK, group * npos), jnp.float32),
+                pltpu.VMEM((n_units, UNIT, group * npos), jnp.float32),
                 pltpu.VMEM((group, 1, LANES), jnp.float32),
                 pltpu.VMEM((group * tp, 1, LANES), jnp.float32),
                 dma((3,)), dma((len(OWN) + n_shared,)),

time: 29.2 us -> 27.7 us (0.949)
  Pallas kernels: 28.5 us -> 27 us
    pallas_call x1, Pallas kernels: 27.8 us -> 26.3 us  [local_part(): pl.pallas_call(functools.partial(head_kernel, group, tp), out_shape=pltpu...]
where the time goes in v6:
time: 27.7 us; the launch traced here: 27.6 us
  Pallas kernels  27 us (97%)
  between operations  0.64 us (2%)
    pallas_call x1, Pallas kernels, local_part(): pl.pallas_call(functools.partial(head_kernel, group, tp), out_shape=pltpu...  26.3 us
    pallas_call x1, Pallas kernels, local_part(): pl.pallas_call(functools.partial(combine_kernel, npos), out_shape=[jax.Sh...  0.69 us

profile of v6, /device:TPU:81, one launch (start us, length us, event | category | flops | bytes accessed | tf_op | source)
XLA Modules:
  0.0 27.6 jit_solution(8697490303440232103)
XLA Ops:
  0.6 26.3 %shard_map.59.got_ref = f32[32,1,128]{2,1,0:T(1,128)S(1)} custom-call(bf16[1,16,2048]{2,1,0:T(8,128)(2,1)} %hid_hbm.1, bf16[2048]{0:T(1024)(128)(2,1)} %w_hbm.1, bf16[32000,2048]{1,0:T(8,128)(2,1)} %emb_hbm.1, s32[1,16]{1,0:T(1,128)} %ids_hbm.1), custom_call_target="tpu_custom_call" | custom-call | tf_op jit(solution)/shard_map/pallas_call | solution.py:315
  26.9 0.7 %shard_map.60 = (f32[1,16]{1,0:T(1,128)}, f32[1,16]{1,0:T(1,128)}) custom-call(f32[32,1,128]{2,1,0:T(1,128)S(1)} %shard_map.59.got_ref), custom_call_target="tpu_custom_call" | custom-call | tf_op jit(solution)/shard_map/pallas_call | solution.py:340

commit v7 on v6

--- a/solution.py
+++ b/solution.py
@@ -13,18 +13,22 @@
 HALVES = 2
 PARTS = 2
 SHARE = 4
-OWN = (1280, 1280)
+OWN = (1024, 1536)
 CHUNK = 1024
-UNIT = 512
-EARLY = 2
-BLOCKS = (1, 1, 1, 1, 2)
+UNIT = 128
+EARLY = 3
+BLOCKS = (1, 2, 2)
 FIRST_LOADS = 1
-SECOND_LOADS = 4
+SECOND_LOADS = 5
 
 
 def shared_chunks(rows):
     sizes = [CHUNK] * (rows // CHUNK)
     return sizes + ([rows % CHUNK] if rows % CHUNK else [])
+
+
+def cut(lo, n):
+    return [(lo + u, min(UNIT, n - u)) for u in range(0, n, UNIT)]
 
 
 def dot_rows(e, h):
@@ -150,21 +154,26 @@
     want_own = jnp.broadcast_to(ids_x[q][:, :npos], (8, npos)) - tp_me * shard - sub
     own = None
 
-    def own_fold(j, own):
-        lo, n = spans[j]
-        return fold(zo[j, :n, :], lo, want_own, own)
+    def own_fold(unit, own):
+        lo, n = unit
+        return fold(zo[lo // UNIT, :n, :], lo, want_own, own)
 
     h_mine = h_own[...]
+    pending = None
     for j in range(len(OWN)):
-        lo, n = spans[j]
+        lo, count = spans[j]
         loads[j].wait()
-        for m, part in enumerate(dot_rows(ebuf.at[pl.ds(lo, n)], h_mine)):
-            zo[j, m * (n // PARTS):(m + 1) * (n // PARTS), :] = part
-        if j:
-            own = own_fold(j - 1, own)
+        for unit in cut(lo, count):
+            lo, n = unit
+            for m, part in enumerate(dot_rows(ebuf.at[pl.ds(lo, n)], h_mine)):
+                zo[lo // UNIT, m * (n // PARTS):(m + 1) * (n // PARTS), :] = part
+            if pending is not None:
+                own = own_fold(pending, own)
+            pending = unit
         if j == 0:
             hear(0)
             tell(1)
+
     for r in others:
         p = member(r)
         direct[r].wait_recv()
@@ -192,10 +201,7 @@
     first_row = tp_me * shard + n_own + q * rows
     want = (want - first_row - lax.broadcasted_iota(jnp.int32, (8, LANES), 0))[:, :width]
 
-    units = []
-    for j in range(len(shared)):
-        lo, n = spans[len(OWN) + j]
-        units.append([(lo + u, min(UNIT, n - u)) for u in range(0, n, UNIT)])
+    units = [cut(*span) for span in spans[len(OWN):]]
     order = [unit for chunk in units for unit in chunk]
 
     def keep(unit, col, width_in, h, add):
@@ -214,7 +220,7 @@
         for unit in units[j]:
             keep(unit, pl.multiple_of(c * half, half), half, h_all[c], False)
         if j == 0:
-            own = own_fold(len(OWN) - 1, own)
+            own = own_fold(pending, own)
 
     mine = (lane >= q * npos) & (lane < (q + 1) * npos)
 
@@ -326,7 +332,7 @@
                 pltpu.VMEM((npos, depth), jnp.bfloat16),
                 pltpu.VMEM((HALVES, group * npos, half), jnp.bfloat16),
                 pltpu.VMEM((sum(OWN) + rows, depth), jnp.bfloat16),
-                pltpu.VMEM((len(OWN), max(OWN), npos), jnp.float32),
+                pltpu.VMEM((sum(OWN) // UNIT, UNIT, npos), jnp.float32),
                 pltpu.VMEM((n_units, UNIT, group * npos), jnp.float32),
                 pltpu.VMEM((group, 1, LANES), jnp.float32),
                 pltpu.VMEM((group * tp, 1, LANES), jnp.float32),

time: 27.7 us -> 27.4 us (0.989)
  Pallas kernels: 27 us -> 26.6 us
    pallas_call x1, Pallas kernels: 26.3 us -> 25.9 us  [local_part(): pl.pallas_call(functools.partial(head_kernel, group, tp), out_shape=pltpu...]
where the time goes in v7:
time: 27.4 us; the launch traced here: 27.3 us
  Pallas kernels  26.6 us (97%)
  between operations  0.64 us (2%)
    pallas_call x1, Pallas kernels, local_part(): pl.pallas_call(functools.partial(head_kernel, group, tp), out_shape=pltpu...  25.9 us
    pallas_call x1, Pallas kernels, local_part(): pl.pallas_call(functools.partial(combine_kernel, npos), out_shape=[jax.Sh...  0.69 us

profile of v7, /device:TPU:81, one launch (start us, length us, event | category | flops | bytes accessed | tf_op | source)
XLA Modules:
  0.0 27.3 jit_solution(5681799843612128447)
XLA Ops:
  0.6 25.9 %shard_map.59.got_ref = f32[32,1,128]{2,1,0:T(1,128)S(1)} custom-call(bf16[1,16,2048]{2,1,0:T(8,128)(2,1)} %hid_hbm.1, bf16[2048]{0:T(1024)(128)(2,1)} %w_hbm.1, bf16[32000,2048]{1,0:T(8,128)(2,1)} %emb_hbm.1, s32[1,16]{1,0:T(1,128)} %ids_hbm.1), custom_call_target="tpu_custom_call" | custom-call | tf_op jit(solution)/shard_map/pallas_call | solution.py:321
  26.6 0.7 %shard_map.60 = (f32[1,16]{1,0:T(1,128)}, f32[1,16]{1,0:T(1,128)}) custom-call(f32[32,1,128]{2,1,0:T(1,128)S(1)} %shard_map.59.got_ref), custom_call_target="tpu_custom_call" | custom-call | tf_op jit(solution)/shard_map/pallas_call | solution.py:346

commit v8 on v7

--- a/solution.py
+++ b/solution.py
@@ -13,11 +13,11 @@
 HALVES = 2
 PARTS = 2
 SHARE = 4
-OWN = (1024, 1536)
+OWN = (1024, 768)
 CHUNK = 1024
 UNIT = 128
-EARLY = 3
-BLOCKS = (1, 2, 2)
+EARLY = 2
+BLOCKS = (2, 2, 2)
 FIRST_LOADS = 1
 SECOND_LOADS = 5
 
@@ -85,6 +85,7 @@
         return lax.rem(q + r, group)
 
     others = tuple(range(group - 1, 0, -1))
+    arrival = (1, 3, 2) if group == 4 else others
 
     small = [
         pltpu.make_async_copy(hid_hbm.at[0], hid_v, in_sem.at[0]),
@@ -174,22 +175,21 @@
             hear(0)
             tell(1)
 
-    for r in others:
+    for s in range(HALVES):
+        place(q, s)
+    for r in arrival:
         p = member(r)
         direct[r].wait_recv()
         forward[r] = pltpu.make_async_remote_copy(
             src_ref=hx.at[p, c], dst_ref=hx.at[p, c], send_sem=f_send.at[r], recv_sem=f_recv.at[r],
             device_id=(dp_me, sibling), device_id_type=MESH)
         forward[r].start()
-    for copy in loads[SECOND_LOADS:]:
-        copy.start()
-    hear(1)
-    tell(2)
+        if r == arrival[-1]:
+            for copy in loads[SECOND_LOADS:]:
+                copy.start()
+        place(p, c)
     for r in others:
         ident[r].wait_recv()
-        place(member(r), c)
-    for s in range(HALVES):
-        place(q, s)
 
     lane = lax.broadcasted_iota(jnp.int32, (8, LANES), 1)
     want = jnp.full((8, LANES), -1, jnp.int32)
@@ -217,6 +217,7 @@
 
     for j in range(EARLY):
         loads[len(OWN) + j].wait()
+    for j in range(EARLY):
         for unit in units[j]:
             keep(unit, pl.multiple_of(c * half, half), half, h_all[c], False)
         if j == 0:
@@ -233,7 +234,8 @@
     for r in others:
         forward[r].wait_recv()
         place(member(r), 1 - c)
-    hear(2)
+    hear(1)
+    tell(2)
     pending = None
     for j in range(EARLY):
         for unit in units[j]:
@@ -253,6 +255,8 @@
                 keep(unit, 0, depth, h_pos, False)
                 state = shared_fold(pending, state)
                 pending = unit
+        if at == EARLY:
+            hear(2)
         at = end
     state = shared_fold(pending, state)
 

time: 27.4 us -> 27 us (0.985)
  Pallas kernels: 26.6 us -> 26.2 us
    pallas_call x1, Pallas kernels: 25.9 us -> 25.6 us  [local_part(): pl.pallas_call(functools.partial(head_kernel, group, tp), out_shape=pltpu...]
where the time goes in v8:
time: 27 us; the launch traced here: 26.9 us
  Pallas kernels  26.2 us (97%)
  between operations  0.64 us (2%)
    pallas_call x1, Pallas kernels, local_part(): pl.pallas_call(functools.partial(head_kernel, group, tp), out_shape=pltpu...  25.6 us
    pallas_call x1, Pallas kernels, local_part(): pl.pallas_call(functools.partial(combine_kernel, npos), out_shape=[jax.Sh...  0.69 us

profile of v8, /device:TPU:81, one launch (start us, length us, event | category | flops | bytes accessed | tf_op | source)
XLA Modules:
  0.0 26.9 jit_solution(4909878812301007190)
XLA Ops:
  0.6 25.6 %shard_map.59.got_ref = f32[32,1,128]{2,1,0:T(1,128)S(1)} custom-call(bf16[1,16,2048]{2,1,0:T(8,128)(2,1)} %hid_hbm.1, bf16[2048]{0:T(1024)(128)(2,1)} %w_hbm.1, bf16[32000,2048]{1,0:T(8,128)(2,1)} %emb_hbm.1, s32[1,16]{1,0:T(1,128)} %ids_hbm.1), custom_call_target="tpu_custom_call" | custom-call | tf_op jit(solution)/shard_map/pallas_call | solution.py:325
  26.2 0.7 %shard_map.60 = (f32[1,16]{1,0:T(1,128)}, f32[1,16]{1,0:T(1,128)}) custom-call(f32[32,1,128]{2,1,0:T(1,128)S(1)} %shard_map.59.got_ref), custom_call_target="tpu_custom_call" | custom-call | tf_op jit(solution)/shard_map/pallas_call | solution.py:350

commit v9 on v8

--- a/solution.py
+++ b/solution.py
@@ -13,11 +13,11 @@
 HALVES = 2
 PARTS = 2
 SHARE = 4
-OWN = (1024, 768)
+OWN = (1024, 1024)
 CHUNK = 1024
 UNIT = 128
 EARLY = 2
-BLOCKS = (2, 2, 2)
+BLOCKS = (1, 2, 3)
 FIRST_LOADS = 1
 SECOND_LOADS = 5
 
@@ -236,6 +236,8 @@
         place(member(r), 1 - c)
     hear(1)
     tell(2)
+    for j in range(EARLY, EARLY + BLOCKS[0]):
+        loads[len(OWN) + j].wait()
     pending = None
     for j in range(EARLY):
         for unit in units[j]:
@@ -248,14 +250,14 @@
     at = EARLY
     for size in BLOCKS:
         end = min(at + size, len(shared))
-        for j in range(at, end):
+        for j in range(max(at, EARLY + BLOCKS[0]), end):
             loads[len(OWN) + j].wait()
         for j in range(at, end):
             for unit in units[j]:
                 keep(unit, 0, depth, h_pos, False)
                 state = shared_fold(pending, state)
                 pending = unit
-        if at == EARLY:
+        if at > EARLY and end < len(shared):
             hear(2)
         at = end
     state = shared_fold(pending, state)

time: 27 us -> 26.8 us (level)
  no operation moved by 1% of the time
where the time goes in v9:
time: 26.8 us; the launch traced here: 26.7 us
  Pallas kernels  26.1 us (97%)
  between operations  0.64 us (2%)
    pallas_call x1, Pallas kernels, local_part(): pl.pallas_call(functools.partial(head_kernel, group, tp), out_shape=pltpu...  25.4 us
    pallas_call x1, Pallas kernels, local_part(): pl.pallas_call(functools.partial(combine_kernel, npos), out_shape=[jax.Sh...  0.69 us

profile of v9, /device:TPU:81, one launch (start us, length us, event | category | flops | bytes accessed | tf_op | source)
XLA Modules:
  0.0 26.7 jit_solution(1265316013037143391)
XLA Ops:
  0.6 25.4 %shard_map.59.got_ref = f32[32,1,128]{2,1,0:T(1,128)S(1)} custom-call(bf16[1,16,2048]{2,1,0:T(8,128)(2,1)} %hid_hbm.1, bf16[2048]{0:T(1024)(128)(2,1)} %w_hbm.1, bf16[32000,2048]{1,0:T(8,128)(2,1)} %emb_hbm.1, s32[1,16]{1,0:T(1,128)} %ids_hbm.1), custom_call_target="tpu_custom_call" | custom-call | tf_op jit(solution)/shard_map/pallas_call | solution.py:327
  26.0 0.7 %shard_map.60 = (f32[1,16]{1,0:T(1,128)}, f32[1,16]{1,0:T(1,128)}) custom-call(f32[32,1,128]{2,1,0:T(1,128)S(1)} %shard_map.59.got_ref), custom_call_target="tpu_custom_call" | custom-call | tf_op jit(solution)/shard_map/pallas_call | solution.py:352
